TPU v7x, 768 devices: a whole 4x8x12 slice. The times are simulated.
768 devices in a mesh: rep: 4 (over y_lo, core), row: 16 (over y_hi, x), col: 12 (over z).
Axes of the slice: x: 4, y: 8 (y_hi: 4, y_lo: 2; y = y_hi * 2 + y_lo), z: 12, core: 2. Of those that a mesh axis runs over, the one named last changes fastest.
Arguments:
- delta: bfloat16 [4, 8192, 4608], P('rep', 'row', 'col'), may hold values from -6 to 6
- params: float32 [8192, 4608], P('row', 'col'), may hold values from -6 to 6
- momentum: float32 [8192, 4608], P('row', 'col'), may hold values from -3 to 3
Outputs:
- params_next: float32 [8192, 4608], P('row', 'col')
- momentum_next: float32 [8192, 4608], P('row', 'col')
- weights: bfloat16 [8192, 4608], P(None, 'col')
All inputs are finite; a program needn't handle non-finite values.
Results may differ from a plain program's by a relative error of at most 0.0075.
Values may be sent and summed in bfloat16 or wider, within the bound.
No kernel may reach another device: no remote copies, remote signals or barrier semaphores. Data moves between devices by JAX's collectives and lax.ppermute only.
A program may use at most 64 MiB of HBM per device.

v0:
```python
import jax
import jax.numpy as jnp
from jax import lax
from jax.experimental import pallas as pl
from jax.experimental.pallas import tpu as pltpu
from jax.sharding import PartitionSpec as P


PLANE = ("rep", "row")
NX, NY = 4, 8


def index(x, y, core):
    return ((y % NY % 2) * 2 + core) * (NX * NY // 2) + (y % NY // 2) * NX + x % NX


def beside(i, core):
    return i + 1 - 2 * ((i + core) % 2)


def send(array, partner):
    pairs = [
        (index(x, y, core), index(*partner(x, y, core)))
        for x in range(NX)
        for y in range(NY)
        for core in range(2)
    ]
    return lax.ppermute(array, PLANE, pairs)


def far_groups():
    return [
        [index(x + 2 * j, y + 2 * i, core) for i in range(NY // 2) for j in range(NX // 2)]
        for x in range(2)
        for y in range(2)
        for core in range(2)
    ]


def update(average, params, momentum):
    momentum_next = 0.9 * momentum + average
    params_next = params - 0.7 * (average + 0.9 * momentum_next)
    return (params_next, momentum_next)


VMEM = pl.BlockSpec(memory_space=pltpu.VMEM)
ANY = pl.BlockSpec(memory_space=pl.ANY)
SMALL = pltpu.CompilerParams(vmem_limit_bytes=8 << 20)


def fetch_kernel(a_ref, b_ref, a_out, b_out, sems):
    copies = [
        pltpu.make_async_copy(a_ref, a_out, sems.at[0]),
        pltpu.make_async_copy(b_ref, b_out, sems.at[1]),
    ]
    for copy in copies:
        copy.start()
    for copy in copies:
        copy.wait()


def fetch(a, b):
    return pl.pallas_call(
        fetch_kernel,
        name="fetch",
        out_shape=(jax.ShapeDtypeStruct(a.shape, a.dtype), jax.ShapeDtypeStruct(b.shape, b.dtype)),
        in_specs=[pl.BlockSpec(memory_space=pltpu.HBM)] * 2,
        out_specs=(VMEM, VMEM),
        scratch_shapes=[pltpu.SemaphoreType.DMA((2,))],
        compiler_params=SMALL,
        cost_estimate=pl.CostEstimate(flops=1000000, bytes_accessed=4 << 20, transcendentals=0),
    )(a, b)


def quarter_kernel(parts_ref, params_ref, momentum_ref, average_ref, weights_ref):
    reps, rows, _ = parts_ref.shape
    at = pl.ds(pl.multiple_of(lax.axis_index("rep") * rows, rows), rows)
    total = parts_ref[0].astype(jnp.float32)
    for i in range(1, reps):
        total += parts_ref[i].astype(jnp.float32)
    average = total / reps
    average_ref[...] = average
    params_next, _ = update(average, params_ref[at], momentum_ref[at])
    for i in range(weights_ref.shape[0]):
        weights_ref[i] = params_next.astype(jnp.bfloat16)


def join_kernel(*refs):
    out_ref, start = refs[-1], 0
    for ref in refs[:-1]:
        out_ref[start : start + ref.shape[0]] = ref[...]
        start += ref.shape[0]


def join(*arrays):
    n = sum(array.shape[0] for array in arrays)
    return pl.pallas_call(
        join_kernel,
        name="join",
        out_shape=jax.ShapeDtypeStruct((n, *arrays[0].shape[1:]), arrays[0].dtype),
        in_specs=[VMEM] * len(arrays),
        out_specs=VMEM,
        compiler_params=SMALL,
    )(*arrays)


def whole_kernel(own_ref, y_ref, swap_ref, params_ref, momentum_ref, params_out, momentum_out):
    rep = lax.axis_index("rep")
    y, core = rep // 2, lax.rem(rep, 2)
    rows = own_ref.shape[0]
    blocks = (
        (y * 2 + core, own_ref[...]),
        ((1 - y) * 2 + core, y_ref[...]),
        (y * 2 + 1 - core, swap_ref[:rows]),
        ((1 - y) * 2 + 1 - core, swap_ref[rows:]),
    )
    for block, average in blocks:
        at = pl.ds(pl.multiple_of(block * rows, rows), rows)
        params_out[at], momentum_out[at] = update(average, params_ref[at], momentum_ref[at])


def place_kernel(spots, *refs):
    out_ref, sems = refs[-2:]
    rep, row = lax.axis_index("rep"), lax.axis_index("row")
    x, y, core = lax.rem(row, 2), rep // 2, lax.rem(rep, 2)
    copies = []
    for ref, spot in zip(refs, spots):
        for i, (k, fx, fy, fc) in enumerate(spot):
            rows = ref.shape[1]
            near = ((1 - x if fx else x) * 2 + (1 - y if fy else y)) * 2 + (1 - core if fc else core)
            at = pl.multiple_of((k * 8 + near) * rows, rows)
            copy = pltpu.make_async_copy(ref.at[i], out_ref.at[pl.ds(at, rows)], sems.at[len(copies)])
            copy.start()
            copies.append(copy)
    for copy in copies:
        copy.wait()


def place(blocks, out, shape):
    arrays, spots = zip(*blocks)
    operands = arrays if out is None else (*arrays, out)
    size = sum(array.size for array in arrays)
    return pl.pallas_call(
        lambda *refs: place_kernel(spots, *refs),
        name="place",
        out_shape=jax.ShapeDtypeStruct(shape, jnp.bfloat16),
        in_specs=[ANY] * len(operands),
        out_specs=ANY,
        scratch_shapes=[pltpu.SemaphoreType.DMA((sum(map(len, spots)),))],
        input_output_aliases={} if out is None else {len(arrays): 0},
        compiler_params=pltpu.CompilerParams(vmem_limit_bytes=1 << 20),
        cost_estimate=pl.CostEstimate(flops=1000000, bytes_accessed=4 * size, transcendentals=0),
    )(*operands)


def on_device(delta, params, momentum):
    reps = lax.axis_size("rep")
    rows, columns = params.shape[0] // reps, params.shape[1]
    groups = far_groups()
    far = len(groups[0])
    block = jax.ShapeDtypeStruct((rows, columns), jnp.float32)
    whole = jax.ShapeDtypeStruct(params.shape, jnp.float32)

    parts = lax.all_to_all(delta[0].reshape(reps, rows, columns), "rep", 0, 0, tiled=True)
    params, momentum = fetch(params, momentum)
    average, weights = pl.pallas_call(
        quarter_kernel,
        name="quarter",
        out_shape=(block, jax.ShapeDtypeStruct((far, rows, columns), jnp.bfloat16)),
        in_specs=[VMEM] * 3,
        out_specs=(VMEM, VMEM),
        compiler_params=SMALL,
    )(parts, params, momentum)

    own = lax.all_to_all(weights, PLANE, 0, 0, axis_index_groups=groups, tiled=True)
    diagonal = lambda x, y, core: (beside(x, core), beside(y, core), core)
    other_core = lambda x, y, core: (x, y, 1 - core)
    by_x = send(own, lambda x, y, core: (beside(x, core), y, core))
    by_y = send(own, lambda x, y, core: (x, beside(y, core), core))
    average_y = send(average, lambda x, y, core: (x, y ^ 1, core))
    both_0 = send(own[: far // 2], diagonal)
    both_1 = send(own[far // 2 :], diagonal)
    average_swap = send(join(average, average_y), other_core)
    near_swap = send(join(own, by_x, by_y), other_core)
    swap_0 = send(both_0, other_core)
    swap_1 = send(both_1, other_core)

    shape = (params.shape[0] * NX * NY // 2, columns)
    spots = lambda fx, fy, fc, ks=range(far): tuple((k, fx, fy, fc) for k in ks)
    first, second = range(far // 2), range(far // 2, far)
    out = place(
        [
            (own, spots(0, 0, 0)),
            (by_x, spots(1, 0, 0)),
            (by_y, spots(0, 1, 0)),
            (near_swap, spots(0, 0, 1) + spots(1, 0, 1) + spots(0, 1, 1)),
        ],
        None,
        shape,
    )
    out = place(
        [
            (both_0, spots(1, 1, 0, first)),
            (both_1, spots(1, 1, 0, second)),
            (swap_0, spots(1, 1, 1, first)),
        ],
        out,
        shape,
    )
    out = place([(swap_1, spots(1, 1, 1, second))], out, shape)

    params_next, momentum_next = pl.pallas_call(
        whole_kernel,
        name="whole",
        out_shape=(whole, whole),
        in_specs=[VMEM] * 5,
        out_specs=(VMEM, VMEM),
        compiler_params=SMALL,
        cost_estimate=pl.CostEstimate(flops=1000000, bytes_accessed=5 << 20, transcendentals=0),
    )(average, average_y, average_swap, params, momentum)
    return (params_next, momentum_next, out)


def solution(mesh):
    return jax.shard_map(
        on_device,
        mesh=mesh,
        in_specs=(P("rep", "row", "col"), P("row", "col"), P("row", "col")),
        out_specs=(P("row", "col"), P("row", "col"), P(None, "col")),
        check_vma=False,
    )
```

profile of v0, /device:TPU:1, one launch (start us, length us, event | category | flops | bytes accessed | tf_op | source)
XLA Modules:
  0.0 97.2 jit_solution(5655089529390260683)
XLA Ops:
  0.6 13.9 %all-to-all-start = ((bf16[4,128,384]{2,1,0:T(8,128)(2,1)}), bf16[4,128,384]{2,1,0:T(8,128)(2,1)S(1)}, u32[]{:S(2)}, u32[]{:S(2)}) async-start(bf16[4,128,384]{2,1,0:T(8,128)(2,1)} %bitcast.1), calls=%async_computation | async-start | bytes 786432 | tf_op jit(solution)/shard_map/all_to_all | solution.py:164
  14.5 1.1 %copy-done = f32[512,384]{1,0:T(8,128)S(1)} copy-done((f32[512,384]{1,0:T(8,128)S(1)}, f32[512,384]{1,0:T(8,128)}, u32[]{:S(2)}) %copy-start) | copy-done | bytes 786456
  15.7 1.1 %copy-done.1 = f32[512,384]{1,0:T(8,128)S(1)} copy-done((f32[512,384]{1,0:T(8,128)S(1)}, f32[512,384]{1,0:T(8,128)}, u32[]{:S(2)}) %copy-start.1) | copy-done | bytes 786456
  16.8 0.1 fetch.1
  16.9 4.0 %all-to-all-done.parts_ref = bf16[4,128,384]{2,1,0:T(8,128)(2,1)S(1)} async-done(((bf16[4,128,384]{2,1,0:T(8,128)(2,1)}), bf16[4,128,384]{2,1,0:T(8,128)(2,1)S(1)}, u32[]{:S(2)}, u32[]{:S(2)}) %all-to-all-start) | async-done | bytes 393248 | tf_op jit(solution)/shard_map/all_to_all | solution.py:164
  21.0 0.1 quarter.1
  21.1 24.8 %all_to_all.10.refs_0_ = bf16[8,128,384]{2,1,0:T(8,128)(2,1)S(1)} all-to-all(bf16[8,128,384]{2,1,0:T(8,128)(2,1)S(1)} %get-tuple-element.14), channel_id=1, replica_groups={{0,24,48,72,96,120,144,168},{192,216,240,264,288,312,336,360},{384,408,..., dimensions={0} | all-to-all | bytes 1572864 | tf_op jit(solution)/shard_map/all_to_all | solution.py:175
  45.9 1.9 %collective-permute-start.6 = (bf16[8,128,384]{2,1,0:T(8,128)(2,1)S(1)}, bf16[8,128,384]{2,1,0:T(8,128)(2,1)S(1)}, u32[]{:S(2)}, u32[]{:S(2)}) collective-permute-start(bf16[8,128,384]{2,1,0:T(8,128)(2,1)S(1)} %all_to_all.10.refs_0_), channel_id=1, source_target_pairs={{0,12},{192,228},{384,396},{576,612},{48,60},{240,276},{432,444},{... | collective-permute-start | bytes 2359304 | tf_op jit(solution)/shard_map/ppermute | solution.py:28
  47.9 1.9 %collective-permute-start.7 = (bf16[8,128,384]{2,1,0:T(8,128)(2,1)S(1)}, bf16[8,128,384]{2,1,0:T(8,128)(2,1)S(1)}, u32[]{:S(2)}, u32[]{:S(2)}) collective-permute-start(bf16[8,128,384]{2,1,0:T(8,128)(2,1)S(1)} %all_to_all.10.refs_0_), channel_id=1, source_target_pairs={{0,384},{192,720},{384,0},{576,240},{48,432},{240,576},{432,48},{6... | collective-permute-start | bytes 2359304 | tf_op jit(solution)/shard_map/ppermute | solution.py:28
  49.8 10.1 %collective-permute-done.6.refs_1_ = bf16[8,128,384]{2,1,0:T(8,128)(2,1)S(1)} collective-permute-done((bf16[8,128,384]{2,1,0:T(8,128)(2,1)S(1)}, bf16[8,128,384]{2,1,0:T(8,128)(2,1)S(1)}, u32[]{:S(2)}, u32[]{:S(2)}) %collective-permute-start.6) | collective-permute-done | bytes 786464 | tf_op jit(solution)/shard_map/ppermute | solution.py:28
  59.9 1.9 %collective-permute-done.7.refs_2_ = bf16[8,128,384]{2,1,0:T(8,128)(2,1)S(1)} collective-permute-done((bf16[8,128,384]{2,1,0:T(8,128)(2,1)S(1)}, bf16[8,128,384]{2,1,0:T(8,128)(2,1)S(1)}, u32[]{:S(2)}, u32[]{:S(2)}) %collective-permute-start.7) | collective-permute-done | bytes 786464 | tf_op jit(solution)/shard_map/ppermute | solution.py:28
  61.8 0.2 join.3
  62.0 3.3 %collective-permute-start.8 = (bf16[24,128,384]{2,1,0:T(8,128)(2,1)S(1)}, bf16[24,128,384]{2,1,0:T(8,128)(2,1)S(1)}, u32[]{:S(2)}, u32[]{:S(2)}) collective-permute-start(bf16[24,128,384]{2,1,0:T(8,128)(2,1)S(1)} %join.3), channel_id=1, source_target_pairs={{0,192},{192,0},{384,576},{576,384},{48,240},{240,48},{432,624},{6... | collective-permute-start | bytes 7077896 | tf_op jit(solution)/shard_map/ppermute | solution.py:28
  65.5 3.2 %collective-permute-start.4 = (bf16[4,128,384]{2,1,0:T(8,128)(2,1)S(1)}, bf16[4,128,384]{2,1,0:T(8,128)(2,1)S(1)}, u32[]{:S(2)}, u32[]{:S(2)}) collective-permute-start(bf16[4,128,384]{2,1,0:T(8,128)(2,1)S(1)} %get-tuple-element.15), channel_id=1, source_target_pairs={{0,396},{192,756},{384,12},{576,276},{48,444},{240,612},{432,60},{... | collective-permute-start | bytes 1179656 | tf_op jit(solution)/shard_map/ppermute | solution.py:28
  68.6 5.4 %collective-permute-start.2 = (bf16[4,128,384]{2,1,0:T(8,128)(2,1)S(1)}, bf16[4,128,384]{2,1,0:T(8,128)(2,1)S(1)}, u32[]{:S(2)}, u32[]{:S(2)}) collective-permute-start(bf16[4,128,384]{2,1,0:T(8,128)(2,1)S(1)} %get-tuple-element.16), channel_id=1, source_target_pairs={{0,396},{192,756},{384,12},{576,276},{48,444},{240,612},{432,60},{... | collective-permute-start | bytes 1179656 | tf_op jit(solution)/shard_map/ppermute | solution.py:28
  74.1 1.9 %collective-permute-start = (f32[128,384]{1,0:T(8,128)S(1)}, f32[128,384]{1,0:T(8,128)S(1)}, u32[]{:S(2)}, u32[]{:S(2)}) collective-permute-start(f32[128,384]{1,0:T(8,128)S(1)} %get-tuple-element.11.refs_0_.own_ref), channel_id=1, source_target_pairs={{0,384},{192,576},{384,0},{576,192},{48,432},{240,624},{432,48},{6... | collective-permute-start | bytes 589832 | tf_op jit(solution)/shard_map/ppermute | solution.py:28
  76.0 6.9 %collective-permute-done.refs_1_.y_ref = f32[128,384]{1,0:T(8,128)S(1)} collective-permute-done((f32[128,384]{1,0:T(8,128)S(1)}, f32[128,384]{1,0:T(8,128)S(1)}, u32[]{:S(2)}, u32[]{:S(2)}) %collective-permute-start) | collective-permute-done | bytes 196640 | tf_op jit(solution)/shard_map/ppermute | solution.py:28
  82.9 4.0 %collective-permute-start.1 = (f32[256,384]{1,0:T(8,128)S(1)}, f32[256,384]{1,0:T(8,128)S(1)}, u32[]{:S(2)}, u32[]{:S(2)}) collective-permute-start(f32[256,384]{1,0:T(8,128)S(1)} %join.2), channel_id=1, source_target_pairs={{0,192},{192,0},{384,576},{576,384},{48,240},{240,48},{432,624},{6... | collective-permute-start | bytes 1179656 | tf_op jit(solution)/shard_map/ppermute | solution.py:28
  87.0 1.9 %collective-permute-start.5 = (bf16[4,128,384]{2,1,0:T(8,128)(2,1)S(1)}, bf16[4,128,384]{2,1,0:T(8,128)(2,1)S(1)}, u32[]{:S(2)}, u32[]{:S(2)}) collective-permute-start(bf16[4,128,384]{2,1,0:T(8,128)(2,1)S(1)} %collective-permute-done.4.refs_0_), channel_id=1, source_target_pairs={{0,192},{192,0},{384,576},{576,384},{48,240},{240,48},{432,624},{6... | collective-permute-start | bytes 1179656 | tf_op jit(solution)/shard_map/ppermute | solution.py:28
  88.9 2.4 %collective-permute-start.3 = (bf16[4,128,384]{2,1,0:T(8,128)(2,1)S(1)}, bf16[4,128,384]{2,1,0:T(8,128)(2,1)S(1)}, u32[]{:S(2)}, u32[]{:S(2)}) collective-permute-start(bf16[4,128,384]{2,1,0:T(8,128)(2,1)S(1)} %collective-permute-done.2.refs_1_), channel_id=1, source_target_pairs={{0,192},{192,0},{384,576},{576,384},{48,240},{240,48},{432,624},{6... | collective-permute-start | bytes 1179656 | tf_op jit(solution)/shard_map/ppermute | solution.py:28
  91.3 1.3 %whole.1 = (f32[512,384]{1,0:T(8,128)}, f32[512,384]{1,0:T(8,128)}) custom-call(f32[128,384]{1,0:T(8,128)S(1)} %get-tuple-element.11.refs_0_.own_ref, f32[128,384]{1,0:T(8,128)S(1)} %collective-permute-done.refs_1_.y_ref, f32[256,384]{1,0:T(8,128)S(1)} %collective-permute-done.1.swap_ref, f32[512,384]{1,0:T(8,128)S(1)} %get-tuple-element.9.params_ref, ...), custom_call_target="tpu_custom_call" | custom-call | flops 1000000 | bytes 5242880 | tf_op jit(solution)/shard_map/whole/pallas_call | solution.py:212
  92.7 2.6 %place.3.refs_3_ = bf16[8192,384]{1,0:T(8,128)(2,1)} custom-call(bf16[8,128,384]{2,1,0:T(8,128)(2,1)S(1)} %all_to_all.10.refs_0_, bf16[8,128,384]{2,1,0:T(8,128)(2,1)S(1)} %collective-permute-done.6.refs_1_, bf16[8,128,384]{2,1,0:T(8,128)(2,1)S(1)} %collective-permute-done.7.refs_2_, bf16[24,128,384]{2,1,0:T(8,128)(2,1)S(1)} %collective-permute-done.8.refs_3_), custom_call_target="tpu_custom_call" | custom-call | flops 1000000 | bytes 9437184 | tf_op jit(solution)/shard_map/place/pallas_call | solution.py:143
  95.3 1.1 %place.4.refs_1_ = bf16[8192,384]{1,0:T(8,128)(2,1)} custom-call(bf16[4,128,384]{2,1,0:T(8,128)(2,1)S(1)} %collective-permute-done.4.refs_0_, bf16[4,128,384]{2,1,0:T(8,128)(2,1)S(1)} %collective-permute-done.2.refs_1_, bf16[4,128,384]{2,1,0:T(8,128)(2,1)S(1)} %collective-permute-done.5.refs_2_, ...), custom_call_target="tpu_custom_call", output_to_operand_aliasing={{}: (3, {})} | custom-call | flops 1000000 | bytes 2359296 | tf_op jit(solution)/shard_map/place/pallas_call | solution.py:143
  96.4 0.8 place.5
  (10 shorter events, 0.1 us)
Async XLA Ops:
  0.6 20.4 %all-to-all-start = ((bf16[4,128,384]{2,1,0:T(8,128)(2,1)}), bf16[4,128,384]{2,1,0:T(8,128)(2,1)S(1)}, u32[]{:S(2)}, u32[]{:S(2)}) async-start(bf16[4,128,384]{2,1,0:T(8,128)(2,1)} %bitcast.1), calls=%async_computation | async-start | bytes 786432 | tf_op jit(solution)/shard_map/all_to_all | solution.py:164
  14.5 1.1 %copy-start = (f32[512,384]{1,0:T(8,128)S(1)}, f32[512,384]{1,0:T(8,128)}, u32[]{:S(2)}) copy-start(f32[512,384]{1,0:T(8,128)} %a_ref.1) | copy-start | bytes 2359300
  15.7 1.1 %copy-start.1 = (f32[512,384]{1,0:T(8,128)S(1)}, f32[512,384]{1,0:T(8,128)}, u32[]{:S(2)}) copy-start(f32[512,384]{1,0:T(8,128)} %b_ref.1) | copy-start | bytes 2359300
  45.9 13.9 %collective-permute-start.6 = (bf16[8,128,384]{2,1,0:T(8,128)(2,1)S(1)}, bf16[8,128,384]{2,1,0:T(8,128)(2,1)S(1)}, u32[]{:S(2)}, u32[]{:S(2)}) collective-permute-start(bf16[8,128,384]{2,1,0:T(8,128)(2,1)S(1)} %all_to_all.10.refs_0_), channel_id=1, source_target_pairs={{0,12},{192,228},{384,396},{576,612},{48,60},{240,276},{432,444},{... | collective-permute-start | bytes 2359304 | tf_op jit(solution)/shard_map/ppermute | solution.py:28
  47.9 13.9 %collective-permute-start.7 = (bf16[8,128,384]{2,1,0:T(8,128)(2,1)S(1)}, bf16[8,128,384]{2,1,0:T(8,128)(2,1)S(1)}, u32[]{:S(2)}, u32[]{:S(2)}) collective-permute-start(bf16[8,128,384]{2,1,0:T(8,128)(2,1)S(1)} %all_to_all.10.refs_0_), channel_id=1, source_target_pairs={{0,384},{192,720},{384,0},{576,240},{48,432},{240,576},{432,48},{6... | collective-permute-start | bytes 2359304 | tf_op jit(solution)/shard_map/ppermute | solution.py:28
  62.0 30.7 %collective-permute-start.8 = (bf16[24,128,384]{2,1,0:T(8,128)(2,1)S(1)}, bf16[24,128,384]{2,1,0:T(8,128)(2,1)S(1)}, u32[]{:S(2)}, u32[]{:S(2)}) collective-permute-start(bf16[24,128,384]{2,1,0:T(8,128)(2,1)S(1)} %join.3), channel_id=1, source_target_pairs={{0,192},{192,0},{384,576},{576,384},{48,240},{240,48},{432,624},{6... | collective-permute-start | bytes 7077896 | tf_op jit(solution)/shard_map/ppermute | solution.py:28
  65.5 21.5 %collective-permute-start.4 = (bf16[4,128,384]{2,1,0:T(8,128)(2,1)S(1)}, bf16[4,128,384]{2,1,0:T(8,128)(2,1)S(1)}, u32[]{:S(2)}, u32[]{:S(2)}) collective-permute-start(bf16[4,128,384]{2,1,0:T(8,128)(2,1)S(1)} %get-tuple-element.15), channel_id=1, source_target_pairs={{0,396},{192,756},{384,12},{576,276},{48,444},{240,612},{432,60},{... | collective-permute-start | bytes 1179656 | tf_op jit(solution)/shard_map/ppermute | solution.py:28
  68.6 20.3 %collective-permute-start.2 = (bf16[4,128,384]{2,1,0:T(8,128)(2,1)S(1)}, bf16[4,128,384]{2,1,0:T(8,128)(2,1)S(1)}, u32[]{:S(2)}, u32[]{:S(2)}) collective-permute-start(bf16[4,128,384]{2,1,0:T(8,128)(2,1)S(1)} %get-tuple-element.16), channel_id=1, source_target_pairs={{0,396},{192,756},{384,12},{576,276},{48,444},{240,612},{432,60},{... | collective-permute-start | bytes 1179656 | tf_op jit(solution)/shard_map/ppermute | solution.py:28
  74.1 8.8 %collective-permute-start = (f32[128,384]{1,0:T(8,128)S(1)}, f32[128,384]{1,0:T(8,128)S(1)}, u32[]{:S(2)}, u32[]{:S(2)}) collective-permute-start(f32[128,384]{1,0:T(8,128)S(1)} %get-tuple-element.11.refs_0_.own_ref), channel_id=1, source_target_pairs={{0,384},{192,576},{384,0},{576,192},{48,432},{240,624},{432,48},{6... | collective-permute-start | bytes 589832 | tf_op jit(solution)/shard_map/ppermute | solution.py:28
  82.9 8.4 %collective-permute-start.1 = (f32[256,384]{1,0:T(8,128)S(1)}, f32[256,384]{1,0:T(8,128)S(1)}, u32[]{:S(2)}, u32[]{:S(2)}) collective-permute-start(f32[256,384]{1,0:T(8,128)S(1)} %join.2), channel_id=1, source_target_pairs={{0,192},{192,0},{384,576},{576,384},{48,240},{240,48},{432,624},{6... | collective-permute-start | bytes 1179656 | tf_op jit(solution)/shard_map/ppermute | solution.py:28
  87.0 8.3 %collective-permute-start.5 = (bf16[4,128,384]{2,1,0:T(8,128)(2,1)S(1)}, bf16[4,128,384]{2,1,0:T(8,128)(2,1)S(1)}, u32[]{:S(2)}, u32[]{:S(2)}) collective-permute-start(bf16[4,128,384]{2,1,0:T(8,128)(2,1)S(1)} %collective-permute-done.4.refs_0_), channel_id=1, source_target_pairs={{0,192},{192,0},{384,576},{576,384},{48,240},{240,48},{432,624},{6... | collective-permute-start | bytes 1179656 | tf_op jit(solution)/shard_map/ppermute | solution.py:28
  88.9 7.5 %collective-permute-start.3 = (bf16[4,128,384]{2,1,0:T(8,128)(2,1)S(1)}, bf16[4,128,384]{2,1,0:T(8,128)(2,1)S(1)}, u32[]{:S(2)}, u32[]{:S(2)}) collective-permute-start(bf16[4,128,384]{2,1,0:T(8,128)(2,1)S(1)} %collective-permute-done.2.refs_1_), channel_id=1, source_target_pairs={{0,192},{192,0},{384,576},{576,384},{48,240},{240,48},{432,624},{6... | collective-permute-start | bytes 1179656 | tf_op jit(solution)/shard_map/ppermute | solution.py:28
where the time goes:
time: 97.8 us; the launch traced here: 97.2 us
  starting transfers between devices  40 us (41%)
  blocking collectives  24.8 us (25%)
  waiting for transfers between devices  23 us (24%)
  Pallas kernels  6.31 us (6%)
  local copies, waits for them, and re-layouts  2.35 us (2%)
    ppermute x9, starting transfers between devices, send(): return lax.ppermute(array, PLANE, pairs)  26.1 us
    all_to_all x1, blocking collectives, on_device(): lax.all_to_all(weights, PLANE, 0, 0, axis_index_groups=groups, tiled=True)  24.8 us
    ppermute x9, waiting for transfers between devices, send(): return lax.ppermute(array, PLANE, pairs)  18.9 us
    all_to_all x1, starting transfers between devices, on_device(): lax.all_to_all(delta[0].reshape(reps, rows, columns), 'rep', 0, 0, tiled=...  13.9 us
    pallas_call x3, Pallas kernels, place(): pl.pallas_call(lambda *refs: place_kernel(spots, *refs), name='place', ou...  4.5 us
    all_to_all x1, waiting for transfers between devices, on_device(): lax.all_to_all(delta[0].reshape(reps, rows, columns), 'rep', 0, 0, tiled=...  4.04 us
    unnamed x4, local copies, waits for them, and re-layouts  2.27 us
  transfers between devices with their start and end apart: 10, of which 4 were waited for; matrix products, arithmetic and copies ran while one was open for 0% of the time, Pallas kernels for 5%

commit v1 on v0

--- a/solution.py
+++ b/solution.py
@@ -48,15 +48,9 @@
 SMALL = pltpu.CompilerParams(vmem_limit_bytes=8 << 20)
 
 
-def fetch_kernel(a_ref, b_ref, a_out, b_out, sems):
-    copies = [
-        pltpu.make_async_copy(a_ref, a_out, sems.at[0]),
-        pltpu.make_async_copy(b_ref, b_out, sems.at[1]),
-    ]
-    for copy in copies:
-        copy.start()
-    for copy in copies:
-        copy.wait()
+def fetch_kernel(a_ref, b_ref, a_out, b_out):
+    a_out[...] = a_ref[...]
+    b_out[...] = b_ref[...]
 
 
 def fetch(a, b):
@@ -64,9 +58,8 @@
         fetch_kernel,
         name="fetch",
         out_shape=(jax.ShapeDtypeStruct(a.shape, a.dtype), jax.ShapeDtypeStruct(b.shape, b.dtype)),
-        in_specs=[pl.BlockSpec(memory_space=pltpu.HBM)] * 2,
+        in_specs=[VMEM] * 2,
         out_specs=(VMEM, VMEM),
-        scratch_shapes=[pltpu.SemaphoreType.DMA((2,))],
         compiler_params=SMALL,
         cost_estimate=pl.CostEstimate(flops=1000000, bytes_accessed=4 << 20, transcendentals=0),
     )(a, b)
@@ -189,24 +182,11 @@
     spots = lambda fx, fy, fc, ks=range(far): tuple((k, fx, fy, fc) for k in ks)
     first, second = range(far // 2), range(far // 2, far)
     out = place(
-        [
-            (own, spots(0, 0, 0)),
-            (by_x, spots(1, 0, 0)),
-            (by_y, spots(0, 1, 0)),
-            (near_swap, spots(0, 0, 1) + spots(1, 0, 1) + spots(0, 1, 1)),
-        ],
-        None,
-        shape,
+        [(own, spots(0, 0, 0)), (by_x, spots(1, 0, 0)), (by_y, spots(0, 1, 0))], None, shape
     )
-    out = place(
-        [
-            (both_0, spots(1, 1, 0, first)),
-            (both_1, spots(1, 1, 0, second)),
-            (swap_0, spots(1, 1, 1, first)),
-        ],
-        out,
-        shape,
-    )
+    swapped = spots(0, 0, 1) + spots(1, 0, 1) + spots(0, 1, 1)
+    out = place([(near_swap, swapped), (both_0, spots(1, 1, 0, first))], out, shape)
+    out = place([(both_1, spots(1, 1, 0, second)), (swap_0, spots(1, 1, 1, first))], out, shape)
     out = place([(swap_1, spots(1, 1, 1, second))], out, shape)
 
     params_next, momentum_next = pl.pallas_call(

time: 97.8 us -> 98.4 us (level)
    pallas_call x3 -> x4, Pallas kernels: 4.5 us -> 5.14 us  [place(): pl.pallas_call(lambda *refs: place_kernel(spots, *refs), name='place', ou...]
  transfers between devices with their start and end apart: 10 -> 10, of which waited for: 4 -> 4; matrix products, arithmetic and copies ran while one was open for 0% -> 0% of each run, Pallas kernels for 5% -> 6%
where the time goes in v1:
time: 98.4 us; the launch traced here: 97.9 us
  starting transfers between devices  40 us (41%)
  blocking collectives  24.8 us (25%)
  waiting for transfers between devices  23 us (23%)
  Pallas kernels  6.94 us (7%)
  local copies, waits for them, and re-layouts  2.35 us (2%)
    ppermute x9, starting transfers between devices, send(): return lax.ppermute(array, PLANE, pairs)  26.1 us
    all_to_all x1, blocking collectives, on_device(): lax.all_to_all(weights, PLANE, 0, 0, axis_index_groups=groups, tiled=True)  24.8 us
    ppermute x9, waiting for transfers between devices, send(): return lax.ppermute(array, PLANE, pairs)  18.9 us
    all_to_all x1, starting transfers between devices, on_device(): lax.all_to_all(delta[0].reshape(reps, rows, columns), 'rep', 0, 0, tiled=...  13.9 us
    pallas_call x4, Pallas kernels, place(): pl.pallas_call(lambda *refs: place_kernel(spots, *refs), name='place', ou...  5.14 us
    all_to_all x1, waiting for transfers between devices, on_device(): lax.all_to_all(delta[0].reshape(reps, rows, columns), 'rep', 0, 0, tiled=...  4.07 us
    unnamed x4, local copies, waits for them, and re-layouts  2.27 us
  transfers between devices with their start and end apart: 10, of which 4 were waited for; matrix products, arithmetic and copies ran while one was open for 0% of the time, Pallas kernels for 6%

profile of v1, /device:TPU:1, one launch (start us, length us, event | category | flops | bytes accessed | tf_op | source)
XLA Modules:
  0.0 97.9 jit_solution(11578507108642565952)
XLA Ops:
  0.6 13.9 %all-to-all-start = ((bf16[4,128,384]{2,1,0:T(8,128)(2,1)}), bf16[4,128,384]{2,1,0:T(8,128)(2,1)S(1)}, u32[]{:S(2)}, u32[]{:S(2)}) async-start(bf16[4,128,384]{2,1,0:T(8,128)(2,1)} %bitcast.1), calls=%async_computation | async-start | bytes 786432 | tf_op jit(solution)/shard_map/all_to_all | solution.py:157
  14.5 1.1 %copy-done = f32[512,384]{1,0:T(8,128)S(1)} copy-done((f32[512,384]{1,0:T(8,128)S(1)}, f32[512,384]{1,0:T(8,128)}, u32[]{:S(2)}) %copy-start) | copy-done | bytes 786456
  15.7 1.1 %copy-done.1 = f32[512,384]{1,0:T(8,128)S(1)} copy-done((f32[512,384]{1,0:T(8,128)S(1)}, f32[512,384]{1,0:T(8,128)}, u32[]{:S(2)}) %copy-start.1) | copy-done | bytes 786456
  16.9 4.1 %all-to-all-done.parts_ref = bf16[4,128,384]{2,1,0:T(8,128)(2,1)S(1)} async-done(((bf16[4,128,384]{2,1,0:T(8,128)(2,1)}), bf16[4,128,384]{2,1,0:T(8,128)(2,1)S(1)}, u32[]{:S(2)}, u32[]{:S(2)}) %all-to-all-start) | async-done | bytes 393248 | tf_op jit(solution)/shard_map/all_to_all | solution.py:157
  21.0 0.1 quarter.1
  21.1 24.8 %all_to_all.10.refs_0_ = bf16[8,128,384]{2,1,0:T(8,128)(2,1)S(1)} all-to-all(bf16[8,128,384]{2,1,0:T(8,128)(2,1)S(1)} %get-tuple-element.14), channel_id=1, replica_groups={{0,24,48,72,96,120,144,168},{192,216,240,264,288,312,336,360},{384,408,..., dimensions={0} | all-to-all | bytes 1572864 | tf_op jit(solution)/shard_map/all_to_all | solution.py:168
  45.9 1.9 %collective-permute-start.6 = (bf16[8,128,384]{2,1,0:T(8,128)(2,1)S(1)}, bf16[8,128,384]{2,1,0:T(8,128)(2,1)S(1)}, u32[]{:S(2)}, u32[]{:S(2)}) collective-permute-start(bf16[8,128,384]{2,1,0:T(8,128)(2,1)S(1)} %all_to_all.10.refs_0_), channel_id=1, source_target_pairs={{0,12},{192,228},{384,396},{576,612},{48,60},{240,276},{432,444},{... | collective-permute-start | bytes 2359304 | tf_op jit(solution)/shard_map/ppermute | solution.py:28
  47.9 1.9 %collective-permute-start.7 = (bf16[8,128,384]{2,1,0:T(8,128)(2,1)S(1)}, bf16[8,128,384]{2,1,0:T(8,128)(2,1)S(1)}, u32[]{:S(2)}, u32[]{:S(2)}) collective-permute-start(bf16[8,128,384]{2,1,0:T(8,128)(2,1)S(1)} %all_to_all.10.refs_0_), channel_id=1, source_target_pairs={{0,384},{192,720},{384,0},{576,240},{48,432},{240,576},{432,48},{6... | collective-permute-start | bytes 2359304 | tf_op jit(solution)/shard_map/ppermute | solution.py:28
  49.8 10.1 %collective-permute-done.6.refs_1_ = bf16[8,128,384]{2,1,0:T(8,128)(2,1)S(1)} collective-permute-done((bf16[8,128,384]{2,1,0:T(8,128)(2,1)S(1)}, bf16[8,128,384]{2,1,0:T(8,128)(2,1)S(1)}, u32[]{:S(2)}, u32[]{:S(2)}) %collective-permute-start.6) | collective-permute-done | bytes 786464 | tf_op jit(solution)/shard_map/ppermute | solution.py:28
  59.9 1.9 %collective-permute-done.7.refs_2_ = bf16[8,128,384]{2,1,0:T(8,128)(2,1)S(1)} collective-permute-done((bf16[8,128,384]{2,1,0:T(8,128)(2,1)S(1)}, bf16[8,128,384]{2,1,0:T(8,128)(2,1)S(1)}, u32[]{:S(2)}, u32[]{:S(2)}) %collective-permute-start.7) | collective-permute-done | bytes 786464 | tf_op jit(solution)/shard_map/ppermute | solution.py:28
  61.8 0.2 join.3
  62.0 3.3 %collective-permute-start.8 = (bf16[24,128,384]{2,1,0:T(8,128)(2,1)S(1)}, bf16[24,128,384]{2,1,0:T(8,128)(2,1)S(1)}, u32[]{:S(2)}, u32[]{:S(2)}) collective-permute-start(bf16[24,128,384]{2,1,0:T(8,128)(2,1)S(1)} %join.3), channel_id=1, source_target_pairs={{0,192},{192,0},{384,576},{576,384},{48,240},{240,48},{432,624},{6... | collective-permute-start | bytes 7077896 | tf_op jit(solution)/shard_map/ppermute | solution.py:28
  65.5 3.2 %collective-permute-start.4 = (bf16[4,128,384]{2,1,0:T(8,128)(2,1)S(1)}, bf16[4,128,384]{2,1,0:T(8,128)(2,1)S(1)}, u32[]{:S(2)}, u32[]{:S(2)}) collective-permute-start(bf16[4,128,384]{2,1,0:T(8,128)(2,1)S(1)} %get-tuple-element.15), channel_id=1, source_target_pairs={{0,396},{192,756},{384,12},{576,276},{48,444},{240,612},{432,60},{... | collective-permute-start | bytes 1179656 | tf_op jit(solution)/shard_map/ppermute | solution.py:28
  68.6 5.4 %collective-permute-start.2 = (bf16[4,128,384]{2,1,0:T(8,128)(2,1)S(1)}, bf16[4,128,384]{2,1,0:T(8,128)(2,1)S(1)}, u32[]{:S(2)}, u32[]{:S(2)}) collective-permute-start(bf16[4,128,384]{2,1,0:T(8,128)(2,1)S(1)} %get-tuple-element.16), channel_id=1, source_target_pairs={{0,396},{192,756},{384,12},{576,276},{48,444},{240,612},{432,60},{... | collective-permute-start | bytes 1179656 | tf_op jit(solution)/shard_map/ppermute | solution.py:28
  74.1 1.9 %collective-permute-start = (f32[128,384]{1,0:T(8,128)S(1)}, f32[128,384]{1,0:T(8,128)S(1)}, u32[]{:S(2)}, u32[]{:S(2)}) collective-permute-start(f32[128,384]{1,0:T(8,128)S(1)} %get-tuple-element.11.refs_0_.own_ref), channel_id=1, source_target_pairs={{0,384},{192,576},{384,0},{576,192},{48,432},{240,624},{432,48},{6... | collective-permute-start | bytes 589832 | tf_op jit(solution)/shard_map/ppermute | solution.py:28
  76.0 6.9 %collective-permute-done.refs_1_.y_ref = f32[128,384]{1,0:T(8,128)S(1)} collective-permute-done((f32[128,384]{1,0:T(8,128)S(1)}, f32[128,384]{1,0:T(8,128)S(1)}, u32[]{:S(2)}, u32[]{:S(2)}) %collective-permute-start) | collective-permute-done | bytes 196640 | tf_op jit(solution)/shard_map/ppermute | solution.py:28
  82.9 4.0 %collective-permute-start.1 = (f32[256,384]{1,0:T(8,128)S(1)}, f32[256,384]{1,0:T(8,128)S(1)}, u32[]{:S(2)}, u32[]{:S(2)}) collective-permute-start(f32[256,384]{1,0:T(8,128)S(1)} %join.2), channel_id=1, source_target_pairs={{0,192},{192,0},{384,576},{576,384},{48,240},{240,48},{432,624},{6... | collective-permute-start | bytes 1179656 | tf_op jit(solution)/shard_map/ppermute | solution.py:28
  87.0 1.9 %collective-permute-start.5 = (bf16[4,128,384]{2,1,0:T(8,128)(2,1)S(1)}, bf16[4,128,384]{2,1,0:T(8,128)(2,1)S(1)}, u32[]{:S(2)}, u32[]{:S(2)}) collective-permute-start(bf16[4,128,384]{2,1,0:T(8,128)(2,1)S(1)} %collective-permute-done.4.refs_1_), channel_id=1, source_target_pairs={{0,192},{192,0},{384,576},{576,384},{48,240},{240,48},{432,624},{6... | collective-permute-start | bytes 1179656 | tf_op jit(solution)/shard_map/ppermute | solution.py:28
  88.9 2.4 %collective-permute-start.3 = (bf16[4,128,384]{2,1,0:T(8,128)(2,1)S(1)}, bf16[4,128,384]{2,1,0:T(8,128)(2,1)S(1)}, u32[]{:S(2)}, u32[]{:S(2)}) collective-permute-start(bf16[4,128,384]{2,1,0:T(8,128)(2,1)S(1)} %collective-permute-done.2.refs_0_), channel_id=1, source_target_pairs={{0,192},{192,0},{384,576},{576,384},{48,240},{240,48},{432,624},{6... | collective-permute-start | bytes 1179656 | tf_op jit(solution)/shard_map/ppermute | solution.py:28
  91.3 1.3 %whole.1 = (f32[512,384]{1,0:T(8,128)}, f32[512,384]{1,0:T(8,128)}) custom-call(f32[128,384]{1,0:T(8,128)S(1)} %get-tuple-element.11.refs_0_.own_ref, f32[128,384]{1,0:T(8,128)S(1)} %collective-permute-done.refs_1_.y_ref, f32[256,384]{1,0:T(8,128)S(1)} %collective-permute-done.1.swap_ref, f32[512,384]{1,0:T(8,128)S(1)} %get-tuple-element.9.params_ref, ...), custom_call_target="tpu_custom_call" | custom-call | flops 1000000 | bytes 5242880 | tf_op jit(solution)/shard_map/whole/pallas_call | solution.py:192
  92.7 1.6 %place.4.refs_2_ = bf16[8192,384]{1,0:T(8,128)(2,1)} custom-call(bf16[8,128,384]{2,1,0:T(8,128)(2,1)S(1)} %all_to_all.10.refs_0_, bf16[8,128,384]{2,1,0:T(8,128)(2,1)S(1)} %collective-permute-done.6.refs_1_, bf16[8,128,384]{2,1,0:T(8,128)(2,1)S(1)} %collective-permute-done.7.refs_2_), custom_call_target="tpu_custom_call" | custom-call | flops 1000000 | bytes 4718592 | tf_op jit(solution)/shard_map/place/pallas_call | solution.py:136
  94.3 1.8 %place.5.refs_2_ = bf16[8192,384]{1,0:T(8,128)(2,1)} custom-call(bf16[24,128,384]{2,1,0:T(8,128)(2,1)S(1)} %collective-permute-done.8.refs_0_, bf16[4,128,384]{2,1,0:T(8,128)(2,1)S(1)} %collective-permute-done.4.refs_1_, bf16[8192,384]{1,0:T(8,128)(2,1)} %place.4.refs_2_), custom_call_target="tpu_custom_call", output_to_operand_aliasing={{}: (2, {})} | custom-call | flops 1000000 | bytes 5505024 | tf_op jit(solution)/shard_map/place/pallas_call | solution.py:136
  96.1 1.0 place.6.refs_1_
  97.1 0.8 place.7
  (11 shorter events, 0.2 us)
Async XLA Ops:
  0.6 20.4 %all-to-all-start = ((bf16[4,128,384]{2,1,0:T(8,128)(2,1)}), bf16[4,128,384]{2,1,0:T(8,128)(2,1)S(1)}, u32[]{:S(2)}, u32[]{:S(2)}) async-start(bf16[4,128,384]{2,1,0:T(8,128)(2,1)} %bitcast.1), calls=%async_computation | async-start | bytes 786432 | tf_op jit(solution)/shard_map/all_to_all | solution.py:157
  14.5 1.1 %copy-start = (f32[512,384]{1,0:T(8,128)S(1)}, f32[512,384]{1,0:T(8,128)}, u32[]{:S(2)}) copy-start(f32[512,384]{1,0:T(8,128)} %a_ref.1) | copy-start | bytes 2359300
  15.7 1.1 %copy-start.1 = (f32[512,384]{1,0:T(8,128)S(1)}, f32[512,384]{1,0:T(8,128)}, u32[]{:S(2)}) copy-start(f32[512,384]{1,0:T(8,128)} %b_ref.1) | copy-start | bytes 2359300
  45.9 13.9 %collective-permute-start.6 = (bf16[8,128,384]{2,1,0:T(8,128)(2,1)S(1)}, bf16[8,128,384]{2,1,0:T(8,128)(2,1)S(1)}, u32[]{:S(2)}, u32[]{:S(2)}) collective-permute-start(bf16[8,128,384]{2,1,0:T(8,128)(2,1)S(1)} %all_to_all.10.refs_0_), channel_id=1, source_target_pairs={{0,12},{192,228},{384,396},{576,612},{48,60},{240,276},{432,444},{... | collective-permute-start | bytes 2359304 | tf_op jit(solution)/shard_map/ppermute | solution.py:28
  47.9 13.9 %collective-permute-start.7 = (bf16[8,128,384]{2,1,0:T(8,128)(2,1)S(1)}, bf16[8,128,384]{2,1,0:T(8,128)(2,1)S(1)}, u32[]{:S(2)}, u32[]{:S(2)}) collective-permute-start(bf16[8,128,384]{2,1,0:T(8,128)(2,1)S(1)} %all_to_all.10.refs_0_), channel_id=1, source_target_pairs={{0,384},{192,720},{384,0},{576,240},{48,432},{240,576},{432,48},{6... | collective-permute-start | bytes 2359304 | tf_op jit(solution)/shard_map/ppermute | solution.py:28
  62.0 32.3 %collective-permute-start.8 = (bf16[24,128,384]{2,1,0:T(8,128)(2,1)S(1)}, bf16[24,128,384]{2,1,0:T(8,128)(2,1)S(1)}, u32[]{:S(2)}, u32[]{:S(2)}) collective-permute-start(bf16[24,128,384]{2,1,0:T(8,128)(2,1)S(1)} %join.3), channel_id=1, source_target_pairs={{0,192},{192,0},{384,576},{576,384},{48,240},{240,48},{432,624},{6... | collective-permute-start | bytes 7077896 | tf_op jit(solution)/shard_map/ppermute | solution.py:28
  65.5 21.5 %collective-permute-start.4 = (bf16[4,128,384]{2,1,0:T(8,128)(2,1)S(1)}, bf16[4,128,384]{2,1,0:T(8,128)(2,1)S(1)}, u32[]{:S(2)}, u32[]{:S(2)}) collective-permute-start(bf16[4,128,384]{2,1,0:T(8,128)(2,1)S(1)} %get-tuple-element.15), channel_id=1, source_target_pairs={{0,396},{192,756},{384,12},{576,276},{48,444},{240,612},{432,60},{... | collective-permute-start | bytes 1179656 | tf_op jit(solution)/shard_map/ppermute | solution.py:28
  68.6 20.3 %collective-permute-start.2 = (bf16[4,128,384]{2,1,0:T(8,128)(2,1)S(1)}, bf16[4,128,384]{2,1,0:T(8,128)(2,1)S(1)}, u32[]{:S(2)}, u32[]{:S(2)}) collective-permute-start(bf16[4,128,384]{2,1,0:T(8,128)(2,1)S(1)} %get-tuple-element.16), channel_id=1, source_target_pairs={{0,396},{192,756},{384,12},{576,276},{48,444},{240,612},{432,60},{... | collective-permute-start | bytes 1179656 | tf_op jit(solution)/shard_map/ppermute | solution.py:28
  74.1 8.8 %collective-permute-start = (f32[128,384]{1,0:T(8,128)S(1)}, f32[128,384]{1,0:T(8,128)S(1)}, u32[]{:S(2)}, u32[]{:S(2)}) collective-permute-start(f32[128,384]{1,0:T(8,128)S(1)} %get-tuple-element.11.refs_0_.own_ref), channel_id=1, source_target_pairs={{0,384},{192,576},{384,0},{576,192},{48,432},{240,624},{432,48},{6... | collective-permute-start | bytes 589832 | tf_op jit(solution)/shard_map/ppermute | solution.py:28
  82.9 8.4 %collective-permute-start.1 = (f32[256,384]{1,0:T(8,128)S(1)}, f32[256,384]{1,0:T(8,128)S(1)}, u32[]{:S(2)}, u32[]{:S(2)}) collective-permute-start(f32[256,384]{1,0:T(8,128)S(1)} %join.2), channel_id=1, source_target_pairs={{0,192},{192,0},{384,576},{576,384},{48,240},{240,48},{432,624},{6... | collective-permute-start | bytes 1179656 | tf_op jit(solution)/shard_map/ppermute | solution.py:28
  87.0 9.1 %collective-permute-start.5 = (bf16[4,128,384]{2,1,0:T(8,128)(2,1)S(1)}, bf16[4,128,384]{2,1,0:T(8,128)(2,1)S(1)}, u32[]{:S(2)}, u32[]{:S(2)}) collective-permute-start(bf16[4,128,384]{2,1,0:T(8,128)(2,1)S(1)} %collective-permute-done.4.refs_1_), channel_id=1, source_target_pairs={{0,192},{192,0},{384,576},{576,384},{48,240},{240,48},{432,624},{6... | collective-permute-start | bytes 1179656 | tf_op jit(solution)/shard_map/ppermute | solution.py:28
  88.9 8.2 %collective-permute-start.3 = (bf16[4,128,384]{2,1,0:T(8,128)(2,1)S(1)}, bf16[4,128,384]{2,1,0:T(8,128)(2,1)S(1)}, u32[]{:S(2)}, u32[]{:S(2)}) collective-permute-start(bf16[4,128,384]{2,1,0:T(8,128)(2,1)S(1)} %collective-permute-done.2.refs_0_), channel_id=1, source_target_pairs={{0,192},{192,0},{384,576},{576,384},{48,240},{240,48},{432,624},{6... | collective-permute-start | bytes 1179656 | tf_op jit(solution)/shard_map/ppermute | solution.py:28

commit v2 on v1

--- a/solution.py
+++ b/solution.py
@@ -151,6 +151,7 @@
     rows, columns = params.shape[0] // reps, params.shape[1]
     groups = far_groups()
     far = len(groups[0])
+    cut = far * 3 // 4
     block = jax.ShapeDtypeStruct((rows, columns), jnp.float32)
     whole = jax.ShapeDtypeStruct(params.shape, jnp.float32)
 
@@ -171,8 +172,8 @@
     by_x = send(own, lambda x, y, core: (beside(x, core), y, core))
     by_y = send(own, lambda x, y, core: (x, beside(y, core), core))
     average_y = send(average, lambda x, y, core: (x, y ^ 1, core))
-    both_0 = send(own[: far // 2], diagonal)
-    both_1 = send(own[far // 2 :], diagonal)
+    both_0 = send(own[:cut], diagonal)
+    both_1 = send(own[cut:], diagonal)
     average_swap = send(join(average, average_y), other_core)
     near_swap = send(join(own, by_x, by_y), other_core)
     swap_0 = send(both_0, other_core)
@@ -180,7 +181,7 @@
 
     shape = (params.shape[0] * NX * NY // 2, columns)
     spots = lambda fx, fy, fc, ks=range(far): tuple((k, fx, fy, fc) for k in ks)
-    first, second = range(far // 2), range(far // 2, far)
+    first, second = range(cut), range(cut, far)
     out = place(
         [(own, spots(0, 0, 0)), (by_x, spots(1, 0, 0)), (by_y, spots(0, 1, 0))], None, shape
     )

time: 98.4 us -> 103 us (1.047)
  waiting for transfers between devices: 23 us -> 30.1 us
  starting transfers between devices: 40 us -> 37.9 us
    ppermute x9, waiting for transfers between devices: 18.9 us -> 26 us  [send(): return lax.ppermute(array, PLANE, pairs)]
    ppermute x9, starting transfers between devices: 26.1 us -> 23.9 us  [send(): return lax.ppermute(array, PLANE, pairs)]
  transfers between devices with their start and end apart: 10 -> 10, of which waited for: 4 -> 5; matrix products, arithmetic and copies ran while one was open for 0% -> 0% of each run, Pallas kernels for 6% -> 6%
where the time goes in v2:
time: 103 us
  starting transfers between devices  37.9 us (37%)
  waiting for transfers between devices  30.1 us (29%)
  blocking collectives  24.8 us (24%)
  Pallas kernels  6.96 us (7%)
  local copies, waits for them, and re-layouts  2.35 us (2%)
    ppermute x9, waiting for transfers between devices, send(): return lax.ppermute(array, PLANE, pairs)  26 us
    all_to_all x1, blocking collectives, on_device(): lax.all_to_all(weights, PLANE, 0, 0, axis_index_groups=groups, tiled=True)  24.8 us
    ppermute x9, starting transfers between devices, send(): return lax.ppermute(array, PLANE, pairs)  23.9 us
    all_to_all x1, starting transfers between devices, on_device(): lax.all_to_all(delta[0].reshape(reps, rows, columns), 'rep', 0, 0, tiled=...  13.9 us
    pallas_call x4, Pallas kernels, place(): pl.pallas_call(lambda *refs: place_kernel(spots, *refs), name='place', ou...  5.14 us
    all_to_all x1, waiting for transfers between devices, on_device(): lax.all_to_all(delta[0].reshape(reps, rows, columns), 'rep', 0, 0, tiled=...  4.07 us
    unnamed x4, local copies, waits for them, and re-layouts  2.27 us
  transfers between devices with their start and end apart: 10, of which 5 were waited for; matrix products, arithmetic and copies ran while one was open for 0% of the time, Pallas kernels for 6%

profile of v2, /device:TPU:1, one launch (start us, length us, event | category | flops | bytes accessed | tf_op | source)
XLA Modules:
  0.0 102.9 jit_solution(3254688311891585651)
XLA Ops:
  0.6 13.9 %all-to-all-start = ((bf16[4,128,384]{2,1,0:T(8,128)(2,1)}), bf16[4,128,384]{2,1,0:T(8,128)(2,1)S(1)}, u32[]{:S(2)}, u32[]{:S(2)}) async-start(bf16[4,128,384]{2,1,0:T(8,128)(2,1)} %bitcast.1), calls=%async_computation | async-start | bytes 786432 | tf_op jit(solution)/shard_map/all_to_all | solution.py:158
  14.5 1.1 %copy-done = f32[512,384]{1,0:T(8,128)S(1)} copy-done((f32[512,384]{1,0:T(8,128)S(1)}, f32[512,384]{1,0:T(8,128)}, u32[]{:S(2)}) %copy-start) | copy-done | bytes 786456
  15.7 1.1 %copy-done.1 = f32[512,384]{1,0:T(8,128)S(1)} copy-done((f32[512,384]{1,0:T(8,128)S(1)}, f32[512,384]{1,0:T(8,128)}, u32[]{:S(2)}) %copy-start.1) | copy-done | bytes 786456
  16.9 4.1 %all-to-all-done.parts_ref = bf16[4,128,384]{2,1,0:T(8,128)(2,1)S(1)} async-done(((bf16[4,128,384]{2,1,0:T(8,128)(2,1)}), bf16[4,128,384]{2,1,0:T(8,128)(2,1)S(1)}, u32[]{:S(2)}, u32[]{:S(2)}) %all-to-all-start) | async-done | bytes 393248 | tf_op jit(solution)/shard_map/all_to_all | solution.py:158
  21.1 24.8 %all_to_all.10.refs_0_ = bf16[8,128,384]{2,1,0:T(8,128)(2,1)S(1)} all-to-all(bf16[8,128,384]{2,1,0:T(8,128)(2,1)S(1)} %get-tuple-element.14), channel_id=1, replica_groups={{0,24,48,72,96,120,144,168},{192,216,240,264,288,312,336,360},{384,408,..., dimensions={0} | all-to-all | bytes 1572864 | tf_op jit(solution)/shard_map/all_to_all | solution.py:169
  45.9 1.9 %collective-permute-start.7 = (bf16[8,128,384]{2,1,0:T(8,128)(2,1)S(1)}, bf16[8,128,384]{2,1,0:T(8,128)(2,1)S(1)}, u32[]{:S(2)}, u32[]{:S(2)}) collective-permute-start(bf16[8,128,384]{2,1,0:T(8,128)(2,1)S(1)} %all_to_all.10.refs_0_), channel_id=1, source_target_pairs={{0,384},{192,720},{384,0},{576,240},{48,432},{240,576},{432,48},{6... | collective-permute-start | bytes 2359304 | tf_op jit(solution)/shard_map/ppermute | solution.py:28
  47.9 1.9 %collective-permute-start.6 = (bf16[8,128,384]{2,1,0:T(8,128)(2,1)S(1)}, bf16[8,128,384]{2,1,0:T(8,128)(2,1)S(1)}, u32[]{:S(2)}, u32[]{:S(2)}) collective-permute-start(bf16[8,128,384]{2,1,0:T(8,128)(2,1)S(1)} %all_to_all.10.refs_0_), channel_id=1, source_target_pairs={{0,12},{192,228},{384,396},{576,612},{48,60},{240,276},{432,444},{... | collective-permute-start | bytes 2359304 | tf_op jit(solution)/shard_map/ppermute | solution.py:28
  49.8 10.1 %collective-permute-done.7.refs_2_ = bf16[8,128,384]{2,1,0:T(8,128)(2,1)S(1)} collective-permute-done((bf16[8,128,384]{2,1,0:T(8,128)(2,1)S(1)}, bf16[8,128,384]{2,1,0:T(8,128)(2,1)S(1)}, u32[]{:S(2)}, u32[]{:S(2)}) %collective-permute-start.7) | collective-permute-done | bytes 786464 | tf_op jit(solution)/shard_map/ppermute | solution.py:28
  59.9 1.9 %collective-permute-done.6.refs_1_ = bf16[8,128,384]{2,1,0:T(8,128)(2,1)S(1)} collective-permute-done((bf16[8,128,384]{2,1,0:T(8,128)(2,1)S(1)}, bf16[8,128,384]{2,1,0:T(8,128)(2,1)S(1)}, u32[]{:S(2)}, u32[]{:S(2)}) %collective-permute-start.6) | collective-permute-done | bytes 786464 | tf_op jit(solution)/shard_map/ppermute | solution.py:28
  61.8 0.2 join.3
  62.0 3.3 %collective-permute-start.8 = (bf16[24,128,384]{2,1,0:T(8,128)(2,1)S(1)}, bf16[24,128,384]{2,1,0:T(8,128)(2,1)S(1)}, u32[]{:S(2)}, u32[]{:S(2)}) collective-permute-start(bf16[24,128,384]{2,1,0:T(8,128)(2,1)S(1)} %join.3), channel_id=1, source_target_pairs={{0,192},{192,0},{384,576},{576,384},{48,240},{240,48},{432,624},{6... | collective-permute-start | bytes 7077896 | tf_op jit(solution)/shard_map/ppermute | solution.py:28
  65.4 3.2 %collective-permute-start.4 = (bf16[6,128,384]{2,1,0:T(8,128)(2,1)S(1)}, bf16[6,128,384]{2,1,0:T(8,128)(2,1)S(1)}, u32[]{:S(2)}, u32[]{:S(2)}) collective-permute-start(bf16[6,128,384]{2,1,0:T(8,128)(2,1)S(1)} %slice.9), channel_id=1, source_target_pairs={{0,396},{192,756},{384,12},{576,276},{48,444},{240,612},{432,60},{... | collective-permute-start | bytes 1769480 | tf_op jit(solution)/shard_map/ppermute | solution.py:28
  68.6 3.2 %collective-permute-start = (f32[128,384]{1,0:T(8,128)S(1)}, f32[128,384]{1,0:T(8,128)S(1)}, u32[]{:S(2)}, u32[]{:S(2)}) collective-permute-start(f32[128,384]{1,0:T(8,128)S(1)} %get-tuple-element.11.refs_0_.own_ref), channel_id=1, source_target_pairs={{0,384},{192,576},{384,0},{576,192},{48,432},{240,624},{432,48},{6... | collective-permute-start | bytes 589832 | tf_op jit(solution)/shard_map/ppermute | solution.py:28
  71.8 7.6 %collective-permute-done.4.refs_1_ = bf16[6,128,384]{2,1,0:T(8,128)(2,1)S(1)} collective-permute-done((bf16[6,128,384]{2,1,0:T(8,128)(2,1)S(1)}, bf16[6,128,384]{2,1,0:T(8,128)(2,1)S(1)}, u32[]{:S(2)}, u32[]{:S(2)}) %collective-permute-start.4) | collective-permute-done | bytes 589856 | tf_op jit(solution)/shard_map/ppermute | solution.py:28
  79.4 2.7 %collective-permute-start.5 = (bf16[6,128,384]{2,1,0:T(8,128)(2,1)S(1)}, bf16[6,128,384]{2,1,0:T(8,128)(2,1)S(1)}, u32[]{:S(2)}, u32[]{:S(2)}) collective-permute-start(bf16[6,128,384]{2,1,0:T(8,128)(2,1)S(1)} %collective-permute-done.4.refs_1_), channel_id=1, source_target_pairs={{0,192},{192,0},{384,576},{576,384},{48,240},{240,48},{432,624},{6... | collective-permute-start | bytes 1769480 | tf_op jit(solution)/shard_map/ppermute | solution.py:28
  82.2 2.4 %collective-permute-start.1 = (f32[256,384]{1,0:T(8,128)S(1)}, f32[256,384]{1,0:T(8,128)S(1)}, u32[]{:S(2)}, u32[]{:S(2)}) collective-permute-start(f32[256,384]{1,0:T(8,128)S(1)} %join.2), channel_id=1, source_target_pairs={{0,192},{192,0},{384,576},{576,384},{48,240},{240,48},{432,624},{6... | collective-permute-start | bytes 1179656 | tf_op jit(solution)/shard_map/ppermute | solution.py:28
  84.6 3.4 %collective-permute-start.2 = (bf16[2,128,384]{2,1,0:T(8,128)(2,1)S(1)}, bf16[2,128,384]{2,1,0:T(8,128)(2,1)S(1)}, u32[]{:S(2)}, u32[]{:S(2)}) collective-permute-start(bf16[2,128,384]{2,1,0:T(8,128)(2,1)S(1)} %slice.8), channel_id=1, source_target_pairs={{0,396},{192,756},{384,12},{576,276},{48,444},{240,612},{432,60},{... | collective-permute-start | bytes 589832 | tf_op jit(solution)/shard_map/ppermute | solution.py:28
  88.0 6.3 %collective-permute-done.2.refs_0_ = bf16[2,128,384]{2,1,0:T(8,128)(2,1)S(1)} collective-permute-done((bf16[2,128,384]{2,1,0:T(8,128)(2,1)S(1)}, bf16[2,128,384]{2,1,0:T(8,128)(2,1)S(1)}, u32[]{:S(2)}, u32[]{:S(2)}) %collective-permute-start.2) | collective-permute-done | bytes 196640 | tf_op jit(solution)/shard_map/ppermute | solution.py:28
  94.4 1.9 %collective-permute-start.3 = (bf16[2,128,384]{2,1,0:T(8,128)(2,1)S(1)}, bf16[2,128,384]{2,1,0:T(8,128)(2,1)S(1)}, u32[]{:S(2)}, u32[]{:S(2)}) collective-permute-start(bf16[2,128,384]{2,1,0:T(8,128)(2,1)S(1)} %collective-permute-done.2.refs_0_), channel_id=1, source_target_pairs={{0,192},{192,0},{384,576},{576,384},{48,240},{240,48},{432,624},{6... | collective-permute-start | bytes 589832 | tf_op jit(solution)/shard_map/ppermute | solution.py:28
  96.3 1.4 %whole.1 = (f32[512,384]{1,0:T(8,128)}, f32[512,384]{1,0:T(8,128)}) custom-call(f32[128,384]{1,0:T(8,128)S(1)} %get-tuple-element.11.refs_0_.own_ref, f32[128,384]{1,0:T(8,128)S(1)} %collective-permute-done.refs_1_.y_ref, f32[256,384]{1,0:T(8,128)S(1)} %collective-permute-done.1.swap_ref, f32[512,384]{1,0:T(8,128)S(1)} %get-tuple-element.9.params_ref, ...), custom_call_target="tpu_custom_call" | custom-call | flops 1000000 | bytes 5242880 | tf_op jit(solution)/shard_map/whole/pallas_call | solution.py:193
  97.7 1.6 %place.4.refs_2_ = bf16[8192,384]{1,0:T(8,128)(2,1)} custom-call(bf16[8,128,384]{2,1,0:T(8,128)(2,1)S(1)} %all_to_all.10.refs_0_, bf16[8,128,384]{2,1,0:T(8,128)(2,1)S(1)} %collective-permute-done.6.refs_1_, bf16[8,128,384]{2,1,0:T(8,128)(2,1)S(1)} %collective-permute-done.7.refs_2_), custom_call_target="tpu_custom_call" | custom-call | flops 1000000 | bytes 4718592 | tf_op jit(solution)/shard_map/place/pallas_call | solution.py:136
  99.3 1.9 %place.5.refs_2_ = bf16[8192,384]{1,0:T(8,128)(2,1)} custom-call(bf16[24,128,384]{2,1,0:T(8,128)(2,1)S(1)} %collective-permute-done.8.refs_0_, bf16[6,128,384]{2,1,0:T(8,128)(2,1)S(1)} %collective-permute-done.4.refs_1_, bf16[8192,384]{1,0:T(8,128)(2,1)} %place.4.refs_2_), custom_call_target="tpu_custom_call", output_to_operand_aliasing={{}: (2, {})} | custom-call | flops 1000000 | bytes 5898240 | tf_op jit(solution)/shard_map/place/pallas_call | solution.py:136
  101.2 1.0 place.6.refs_1_
  102.2 0.7 place.7
  (12 shorter events, 0.3 us)
Async XLA Ops:
  0.6 20.4 %all-to-all-start = ((bf16[4,128,384]{2,1,0:T(8,128)(2,1)}), bf16[4,128,384]{2,1,0:T(8,128)(2,1)S(1)}, u32[]{:S(2)}, u32[]{:S(2)}) async-start(bf16[4,128,384]{2,1,0:T(8,128)(2,1)} %bitcast.1), calls=%async_computation | async-start | bytes 786432 | tf_op jit(solution)/shard_map/all_to_all | solution.py:158
  14.5 1.1 %copy-start = (f32[512,384]{1,0:T(8,128)S(1)}, f32[512,384]{1,0:T(8,128)}, u32[]{:S(2)}) copy-start(f32[512,384]{1,0:T(8,128)} %a_ref.1) | copy-start | bytes 2359300
  15.7 1.1 %copy-start.1 = (f32[512,384]{1,0:T(8,128)S(1)}, f32[512,384]{1,0:T(8,128)}, u32[]{:S(2)}) copy-start(f32[512,384]{1,0:T(8,128)} %b_ref.1) | copy-start | bytes 2359300
  45.9 13.9 %collective-permute-start.7 = (bf16[8,128,384]{2,1,0:T(8,128)(2,1)S(1)}, bf16[8,128,384]{2,1,0:T(8,128)(2,1)S(1)}, u32[]{:S(2)}, u32[]{:S(2)}) collective-permute-start(bf16[8,128,384]{2,1,0:T(8,128)(2,1)S(1)} %all_to_all.10.refs_0_), channel_id=1, source_target_pairs={{0,384},{192,720},{384,0},{576,240},{48,432},{240,576},{432,48},{6... | collective-permute-start | bytes 2359304 | tf_op jit(solution)/shard_map/ppermute | solution.py:28
  47.9 13.9 %collective-permute-start.6 = (bf16[8,128,384]{2,1,0:T(8,128)(2,1)S(1)}, bf16[8,128,384]{2,1,0:T(8,128)(2,1)S(1)}, u32[]{:S(2)}, u32[]{:S(2)}) collective-permute-start(bf16[8,128,384]{2,1,0:T(8,128)(2,1)S(1)} %all_to_all.10.refs_0_), channel_id=1, source_target_pairs={{0,12},{192,228},{384,396},{576,612},{48,60},{240,276},{432,444},{... | collective-permute-start | bytes 2359304 | tf_op jit(solution)/shard_map/ppermute | solution.py:28
  62.0 37.3 %collective-permute-start.8 = (bf16[24,128,384]{2,1,0:T(8,128)(2,1)S(1)}, bf16[24,128,384]{2,1,0:T(8,128)(2,1)S(1)}, u32[]{:S(2)}, u32[]{:S(2)}) collective-permute-start(bf16[24,128,384]{2,1,0:T(8,128)(2,1)S(1)} %join.3), channel_id=1, source_target_pairs={{0,192},{192,0},{384,576},{576,384},{48,240},{240,48},{432,624},{6... | collective-permute-start | bytes 7077896 | tf_op jit(solution)/shard_map/ppermute | solution.py:28
  65.4 13.9 %collective-permute-start.4 = (bf16[6,128,384]{2,1,0:T(8,128)(2,1)S(1)}, bf16[6,128,384]{2,1,0:T(8,128)(2,1)S(1)}, u32[]{:S(2)}, u32[]{:S(2)}) collective-permute-start(bf16[6,128,384]{2,1,0:T(8,128)(2,1)S(1)} %slice.9), channel_id=1, source_target_pairs={{0,396},{192,756},{384,12},{576,276},{48,444},{240,612},{432,60},{... | collective-permute-start | bytes 1769480 | tf_op jit(solution)/shard_map/ppermute | solution.py:28
  68.6 13.5 %collective-permute-start = (f32[128,384]{1,0:T(8,128)S(1)}, f32[128,384]{1,0:T(8,128)S(1)}, u32[]{:S(2)}, u32[]{:S(2)}) collective-permute-start(f32[128,384]{1,0:T(8,128)S(1)} %get-tuple-element.11.refs_0_.own_ref), channel_id=1, source_target_pairs={{0,384},{192,576},{384,0},{576,192},{48,432},{240,624},{432,48},{6... | collective-permute-start | bytes 589832 | tf_op jit(solution)/shard_map/ppermute | solution.py:28
  79.4 21.8 %collective-permute-start.5 = (bf16[6,128,384]{2,1,0:T(8,128)(2,1)S(1)}, bf16[6,128,384]{2,1,0:T(8,128)(2,1)S(1)}, u32[]{:S(2)}, u32[]{:S(2)}) collective-permute-start(bf16[6,128,384]{2,1,0:T(8,128)(2,1)S(1)} %collective-permute-done.4.refs_1_), channel_id=1, source_target_pairs={{0,192},{192,0},{384,576},{576,384},{48,240},{240,48},{432,624},{6... | collective-permute-start | bytes 1769480 | tf_op jit(solution)/shard_map/ppermute | solution.py:28
  82.2 14.1 %collective-permute-start.1 = (f32[256,384]{1,0:T(8,128)S(1)}, f32[256,384]{1,0:T(8,128)S(1)}, u32[]{:S(2)}, u32[]{:S(2)}) collective-permute-start(f32[256,384]{1,0:T(8,128)S(1)} %join.2), channel_id=1, source_target_pairs={{0,192},{192,0},{384,576},{576,384},{48,240},{240,48},{432,624},{6... | collective-permute-start | bytes 1179656 | tf_op jit(solution)/shard_map/ppermute | solution.py:28
  84.6 9.7 %collective-permute-start.2 = (bf16[2,128,384]{2,1,0:T(8,128)(2,1)S(1)}, bf16[2,128,384]{2,1,0:T(8,128)(2,1)S(1)}, u32[]{:S(2)}, u32[]{:S(2)}) collective-permute-start(bf16[2,128,384]{2,1,0:T(8,128)(2,1)S(1)} %slice.8), channel_id=1, source_target_pairs={{0,396},{192,756},{384,12},{576,276},{48,444},{240,612},{432,60},{... | collective-permute-start | bytes 589832 | tf_op jit(solution)/shard_map/ppermute | solution.py:28
  94.4 7.8 %collective-permute-start.3 = (bf16[2,128,384]{2,1,0:T(8,128)(2,1)S(1)}, bf16[2,128,384]{2,1,0:T(8,128)(2,1)S(1)}, u32[]{:S(2)}, u32[]{:S(2)}) collective-permute-start(bf16[2,128,384]{2,1,0:T(8,128)(2,1)S(1)} %collective-permute-done.2.refs_0_), channel_id=1, source_target_pairs={{0,192},{192,0},{384,576},{576,384},{48,240},{240,48},{432,624},{6... | collective-permute-start | bytes 589832 | tf_op jit(solution)/shard_map/ppermute | solution.py:28

commit v3 on v1

--- a/solution.py
+++ b/solution.py
@@ -171,23 +171,20 @@
     by_x = send(own, lambda x, y, core: (beside(x, core), y, core))
     by_y = send(own, lambda x, y, core: (x, beside(y, core), core))
     average_y = send(average, lambda x, y, core: (x, y ^ 1, core))
-    both_0 = send(own[: far // 2], diagonal)
-    both_1 = send(own[far // 2 :], diagonal)
+    both = send(own, diagonal)
     average_swap = send(join(average, average_y), other_core)
     near_swap = send(join(own, by_x, by_y), other_core)
-    swap_0 = send(both_0, other_core)
-    swap_1 = send(both_1, other_core)
+    both_swap = send(both, other_core)
 
     shape = (params.shape[0] * NX * NY // 2, columns)
-    spots = lambda fx, fy, fc, ks=range(far): tuple((k, fx, fy, fc) for k in ks)
-    first, second = range(far // 2), range(far // 2, far)
+    spots = lambda fx, fy, fc: tuple((k, fx, fy, fc) for k in range(far))
     out = place(
         [(own, spots(0, 0, 0)), (by_x, spots(1, 0, 0)), (by_y, spots(0, 1, 0))], None, shape
     )
     swapped = spots(0, 0, 1) + spots(1, 0, 1) + spots(0, 1, 1)
-    out = place([(near_swap, swapped), (both_0, spots(1, 1, 0, first))], out, shape)
-    out = place([(both_1, spots(1, 1, 0, second)), (swap_0, spots(1, 1, 1, first))], out, shape)
-    out = place([(swap_1, spots(1, 1, 1, second))], out, shape)
+    out = place([(near_swap, swapped)], out, shape)
+    out = place([(both, spots(1, 1, 0))], out, shape)
+    out = place([(both_swap, spots(1, 1, 1))], out, shape)
 
     params_next, momentum_next = pl.pallas_call(
         whole_kernel,

time: 98.4 us -> 103 us (1.047)
  waiting for transfers between devices: 23 us -> 36.2 us
  starting transfers between devices: 40 us -> 31.3 us
    ppermute x9 -> x7, waiting for transfers between devices: 18.9 us -> 32.2 us  [send(): return lax.ppermute(array, PLANE, pairs)]
    ppermute x9 -> x7, starting transfers between devices: 26.1 us -> 17.4 us  [send(): return lax.ppermute(array, PLANE, pairs)]
  transfers between devices with their start and end apart: 10 -> 8, of which waited for: 4 -> 6; matrix products, arithmetic and copies ran while one was open for 0% -> 0% of each run, Pallas kernels for 6% -> 6%
where the time goes in v3:
time: 103 us; the launch traced here: 102 us
  waiting for transfers between devices  36.2 us (35%)
  starting transfers between devices  31.3 us (30%)
  blocking collectives  24.8 us (24%)
  Pallas kernels  6.91 us (7%)
  local copies, waits for them, and re-layouts  2.27 us (2%)
    ppermute x7, waiting for transfers between devices, send(): return lax.ppermute(array, PLANE, pairs)  32.2 us
    all_to_all x1, blocking collectives, on_device(): lax.all_to_all(weights, PLANE, 0, 0, axis_index_groups=groups, tiled=True)  24.8 us
    ppermute x7, starting transfers between devices, send(): return lax.ppermute(array, PLANE, pairs)  17.4 us
    all_to_all x1, starting transfers between devices, on_device(): lax.all_to_all(delta[0].reshape(reps, rows, columns), 'rep', 0, 0, tiled=...  13.9 us
    pallas_call x4, Pallas kernels, place(): pl.pallas_call(lambda *refs: place_kernel(spots, *refs), name='place', ou...  5.14 us
    all_to_all x1, waiting for transfers between devices, on_device(): lax.all_to_all(delta[0].reshape(reps, rows, columns), 'rep', 0, 0, tiled=...  4.07 us
    unnamed x4, local copies, waits for them, and re-layouts  2.27 us
  transfers between devices with their start and end apart: 8, of which 6 were waited for; matrix products, arithmetic and copies ran while one was open for 0% of the time, Pallas kernels for 6%

profile of v3, /device:TPU:1, one launch (start us, length us, event | category | flops | bytes accessed | tf_op | source)
XLA Modules:
  0.0 102.3 jit_solution(16280446693823468963)
XLA Ops:
  0.6 13.9 %all-to-all-start = ((bf16[4,128,384]{2,1,0:T(8,128)(2,1)}), bf16[4,128,384]{2,1,0:T(8,128)(2,1)S(1)}, u32[]{:S(2)}, u32[]{:S(2)}) async-start(bf16[4,128,384]{2,1,0:T(8,128)(2,1)} %bitcast.1), calls=%async_computation | async-start | bytes 786432 | tf_op jit(solution)/shard_map/all_to_all | solution.py:157
  14.5 1.1 %copy-done = f32[512,384]{1,0:T(8,128)S(1)} copy-done((f32[512,384]{1,0:T(8,128)S(1)}, f32[512,384]{1,0:T(8,128)}, u32[]{:S(2)}) %copy-start) | copy-done | bytes 786456
  15.7 1.1 %copy-done.1 = f32[512,384]{1,0:T(8,128)S(1)} copy-done((f32[512,384]{1,0:T(8,128)S(1)}, f32[512,384]{1,0:T(8,128)}, u32[]{:S(2)}) %copy-start.1) | copy-done | bytes 786456
  16.9 4.1 %all-to-all-done.parts_ref = bf16[4,128,384]{2,1,0:T(8,128)(2,1)S(1)} async-done(((bf16[4,128,384]{2,1,0:T(8,128)(2,1)}), bf16[4,128,384]{2,1,0:T(8,128)(2,1)S(1)}, u32[]{:S(2)}, u32[]{:S(2)}) %all-to-all-start) | async-done | bytes 393248 | tf_op jit(solution)/shard_map/all_to_all | solution.py:157
  21.0 0.1 quarter.1
  21.1 24.8 %all_to_all.10.refs_0_ = bf16[8,128,384]{2,1,0:T(8,128)(2,1)S(1)} all-to-all(bf16[8,128,384]{2,1,0:T(8,128)(2,1)S(1)} %get-tuple-element.14), channel_id=1, replica_groups={{0,24,48,72,96,120,144,168},{192,216,240,264,288,312,336,360},{384,408,..., dimensions={0} | all-to-all | bytes 1572864 | tf_op jit(solution)/shard_map/all_to_all | solution.py:168
  45.9 1.9 %collective-permute-start.4 = (bf16[8,128,384]{2,1,0:T(8,128)(2,1)S(1)}, bf16[8,128,384]{2,1,0:T(8,128)(2,1)S(1)}, u32[]{:S(2)}, u32[]{:S(2)}) collective-permute-start(bf16[8,128,384]{2,1,0:T(8,128)(2,1)S(1)} %all_to_all.10.refs_0_), channel_id=1, source_target_pairs={{0,12},{192,228},{384,396},{576,612},{48,60},{240,276},{432,444},{... | collective-permute-start | bytes 2359304 | tf_op jit(solution)/shard_map/ppermute | solution.py:28
  47.9 1.9 %collective-permute-start.5 = (bf16[8,128,384]{2,1,0:T(8,128)(2,1)S(1)}, bf16[8,128,384]{2,1,0:T(8,128)(2,1)S(1)}, u32[]{:S(2)}, u32[]{:S(2)}) collective-permute-start(bf16[8,128,384]{2,1,0:T(8,128)(2,1)S(1)} %all_to_all.10.refs_0_), channel_id=1, source_target_pairs={{0,384},{192,720},{384,0},{576,240},{48,432},{240,576},{432,48},{6... | collective-permute-start | bytes 2359304 | tf_op jit(solution)/shard_map/ppermute | solution.py:28
  49.8 10.1 %collective-permute-done.4.refs_1_ = bf16[8,128,384]{2,1,0:T(8,128)(2,1)S(1)} collective-permute-done((bf16[8,128,384]{2,1,0:T(8,128)(2,1)S(1)}, bf16[8,128,384]{2,1,0:T(8,128)(2,1)S(1)}, u32[]{:S(2)}, u32[]{:S(2)}) %collective-permute-start.4) | collective-permute-done | bytes 786464 | tf_op jit(solution)/shard_map/ppermute | solution.py:28
  59.9 1.9 %collective-permute-done.5.refs_2_ = bf16[8,128,384]{2,1,0:T(8,128)(2,1)S(1)} collective-permute-done((bf16[8,128,384]{2,1,0:T(8,128)(2,1)S(1)}, bf16[8,128,384]{2,1,0:T(8,128)(2,1)S(1)}, u32[]{:S(2)}, u32[]{:S(2)}) %collective-permute-start.5) | collective-permute-done | bytes 786464 | tf_op jit(solution)/shard_map/ppermute | solution.py:28
  61.8 0.2 join.3
  62.0 3.3 %collective-permute-start.6 = (bf16[24,128,384]{2,1,0:T(8,128)(2,1)S(1)}, bf16[24,128,384]{2,1,0:T(8,128)(2,1)S(1)}, u32[]{:S(2)}, u32[]{:S(2)}) collective-permute-start(bf16[24,128,384]{2,1,0:T(8,128)(2,1)S(1)} %join.3), channel_id=1, source_target_pairs={{0,192},{192,0},{384,576},{576,384},{48,240},{240,48},{432,624},{6... | collective-permute-start | bytes 7077896 | tf_op jit(solution)/shard_map/ppermute | solution.py:28
  65.4 3.2 %collective-permute-start.2 = (bf16[8,128,384]{2,1,0:T(8,128)(2,1)S(1)}, bf16[8,128,384]{2,1,0:T(8,128)(2,1)S(1)}, u32[]{:S(2)}, u32[]{:S(2)}) collective-permute-start(bf16[8,128,384]{2,1,0:T(8,128)(2,1)S(1)} %all_to_all.10.refs_0_), channel_id=1, source_target_pairs={{0,396},{192,756},{384,12},{576,276},{48,444},{240,612},{432,60},{... | collective-permute-start | bytes 2359304 | tf_op jit(solution)/shard_map/ppermute | solution.py:28
  68.5 12.9 %collective-permute-done.2.refs_0_ = bf16[8,128,384]{2,1,0:T(8,128)(2,1)S(1)} collective-permute-done((bf16[8,128,384]{2,1,0:T(8,128)(2,1)S(1)}, bf16[8,128,384]{2,1,0:T(8,128)(2,1)S(1)}, u32[]{:S(2)}, u32[]{:S(2)}) %collective-permute-start.2) | collective-permute-done | bytes 786464 | tf_op jit(solution)/shard_map/ppermute | solution.py:28
  81.4 1.9 %collective-permute-start.3 = (bf16[8,128,384]{2,1,0:T(8,128)(2,1)S(1)}, bf16[8,128,384]{2,1,0:T(8,128)(2,1)S(1)}, u32[]{:S(2)}, u32[]{:S(2)}) collective-permute-start(bf16[8,128,384]{2,1,0:T(8,128)(2,1)S(1)} %collective-permute-done.2.refs_0_), channel_id=1, source_target_pairs={{0,192},{192,0},{384,576},{576,384},{48,240},{240,48},{432,624},{6... | collective-permute-start | bytes 2359304 | tf_op jit(solution)/shard_map/ppermute | solution.py:28
  83.3 1.9 %collective-permute-start = (f32[128,384]{1,0:T(8,128)S(1)}, f32[128,384]{1,0:T(8,128)S(1)}, u32[]{:S(2)}, u32[]{:S(2)}) collective-permute-start(f32[128,384]{1,0:T(8,128)S(1)} %get-tuple-element.11.refs_0_.own_ref), channel_id=1, source_target_pairs={{0,384},{192,576},{384,0},{576,192},{48,432},{240,624},{432,48},{6... | collective-permute-start | bytes 589832 | tf_op jit(solution)/shard_map/ppermute | solution.py:28
  85.3 5.9 %collective-permute-done.refs_1_.y_ref = f32[128,384]{1,0:T(8,128)S(1)} collective-permute-done((f32[128,384]{1,0:T(8,128)S(1)}, f32[128,384]{1,0:T(8,128)S(1)}, u32[]{:S(2)}, u32[]{:S(2)}) %collective-permute-start) | collective-permute-done | bytes 196640 | tf_op jit(solution)/shard_map/ppermute | solution.py:28
  91.2 3.3 %collective-permute-start.1 = (f32[256,384]{1,0:T(8,128)S(1)}, f32[256,384]{1,0:T(8,128)S(1)}, u32[]{:S(2)}, u32[]{:S(2)}) collective-permute-start(f32[256,384]{1,0:T(8,128)S(1)} %join.2), channel_id=1, source_target_pairs={{0,192},{192,0},{384,576},{576,384},{48,240},{240,48},{432,624},{6... | collective-permute-start | bytes 1179656 | tf_op jit(solution)/shard_map/ppermute | solution.py:28
  94.5 1.3 %collective-permute-done.1.swap_ref = f32[256,384]{1,0:T(8,128)S(1)} collective-permute-done((f32[256,384]{1,0:T(8,128)S(1)}, f32[256,384]{1,0:T(8,128)S(1)}, u32[]{:S(2)}, u32[]{:S(2)}) %collective-permute-start.1) | collective-permute-done | bytes 393248 | tf_op jit(solution)/shard_map/ppermute | solution.py:28
  95.8 1.3 %whole.1 = (f32[512,384]{1,0:T(8,128)}, f32[512,384]{1,0:T(8,128)}) custom-call(f32[128,384]{1,0:T(8,128)S(1)} %get-tuple-element.11.refs_0_.own_ref, f32[128,384]{1,0:T(8,128)S(1)} %collective-permute-done.refs_1_.y_ref, f32[256,384]{1,0:T(8,128)S(1)} %collective-permute-done.1.swap_ref, f32[512,384]{1,0:T(8,128)S(1)} %get-tuple-element.9.params_ref, ...), custom_call_target="tpu_custom_call" | custom-call | flops 1000000 | bytes 5242880 | tf_op jit(solution)/shard_map/whole/pallas_call | solution.py:189
  97.2 1.6 %place.4.refs_1_ = bf16[8192,384]{1,0:T(8,128)(2,1)} custom-call(bf16[8,128,384]{2,1,0:T(8,128)(2,1)S(1)} %all_to_all.10.refs_0_, bf16[8,128,384]{2,1,0:T(8,128)(2,1)S(1)} %collective-permute-done.4.refs_1_, bf16[8,128,384]{2,1,0:T(8,128)(2,1)S(1)} %collective-permute-done.5.refs_2_), custom_call_target="tpu_custom_call" | custom-call | flops 1000000 | bytes 4718592 | tf_op jit(solution)/shard_map/place/pallas_call | solution.py:136
  98.8 1.6 %place.5.refs_1_ = bf16[8192,384]{1,0:T(8,128)(2,1)} custom-call(bf16[24,128,384]{2,1,0:T(8,128)(2,1)S(1)} %collective-permute-done.6.refs_0_, bf16[8192,384]{1,0:T(8,128)(2,1)} %place.4.refs_1_), custom_call_target="tpu_custom_call", output_to_operand_aliasing={{}: (1, {})} | custom-call | flops 1000000 | bytes 4718592 | tf_op jit(solution)/shard_map/place/pallas_call | solution.py:136
  100.4 1.0 place.6.refs_1_
  101.4 1.0 place.7
  (6 shorter events, 0.1 us)
Async XLA Ops:
  0.6 20.4 %all-to-all-start = ((bf16[4,128,384]{2,1,0:T(8,128)(2,1)}), bf16[4,128,384]{2,1,0:T(8,128)(2,1)S(1)}, u32[]{:S(2)}, u32[]{:S(2)}) async-start(bf16[4,128,384]{2,1,0:T(8,128)(2,1)} %bitcast.1), calls=%async_computation | async-start | bytes 786432 | tf_op jit(solution)/shard_map/all_to_all | solution.py:157
  14.5 1.1 %copy-start = (f32[512,384]{1,0:T(8,128)S(1)}, f32[512,384]{1,0:T(8,128)}, u32[]{:S(2)}) copy-start(f32[512,384]{1,0:T(8,128)} %a_ref.1) | copy-start | bytes 2359300
  15.7 1.1 %copy-start.1 = (f32[512,384]{1,0:T(8,128)S(1)}, f32[512,384]{1,0:T(8,128)}, u32[]{:S(2)}) copy-start(f32[512,384]{1,0:T(8,128)} %b_ref.1) | copy-start | bytes 2359300
  45.9 13.9 %collective-permute-start.4 = (bf16[8,128,384]{2,1,0:T(8,128)(2,1)S(1)}, bf16[8,128,384]{2,1,0:T(8,128)(2,1)S(1)}, u32[]{:S(2)}, u32[]{:S(2)}) collective-permute-start(bf16[8,128,384]{2,1,0:T(8,128)(2,1)S(1)} %all_to_all.10.refs_0_), channel_id=1, source_target_pairs={{0,12},{192,228},{384,396},{576,612},{48,60},{240,276},{432,444},{... | collective-permute-start | bytes 2359304 | tf_op jit(solution)/shard_map/ppermute | solution.py:28
  47.9 13.9 %collective-permute-start.5 = (bf16[8,128,384]{2,1,0:T(8,128)(2,1)S(1)}, bf16[8,128,384]{2,1,0:T(8,128)(2,1)S(1)}, u32[]{:S(2)}, u32[]{:S(2)}) collective-permute-start(bf16[8,128,384]{2,1,0:T(8,128)(2,1)S(1)} %all_to_all.10.refs_0_), channel_id=1, source_target_pairs={{0,384},{192,720},{384,0},{576,240},{48,432},{240,576},{432,48},{6... | collective-permute-start | bytes 2359304 | tf_op jit(solution)/shard_map/ppermute | solution.py:28
  62.0 36.7 %collective-permute-start.6 = (bf16[24,128,384]{2,1,0:T(8,128)(2,1)S(1)}, bf16[24,128,384]{2,1,0:T(8,128)(2,1)S(1)}, u32[]{:S(2)}, u32[]{:S(2)}) collective-permute-start(bf16[24,128,384]{2,1,0:T(8,128)(2,1)S(1)} %join.3), channel_id=1, source_target_pairs={{0,192},{192,0},{384,576},{576,384},{48,240},{240,48},{432,624},{6... | collective-permute-start | bytes 7077896 | tf_op jit(solution)/shard_map/ppermute | solution.py:28
  65.4 16.1 %collective-permute-start.2 = (bf16[8,128,384]{2,1,0:T(8,128)(2,1)S(1)}, bf16[8,128,384]{2,1,0:T(8,128)(2,1)S(1)}, u32[]{:S(2)}, u32[]{:S(2)}) collective-permute-start(bf16[8,128,384]{2,1,0:T(8,128)(2,1)S(1)} %all_to_all.10.refs_0_), channel_id=1, source_target_pairs={{0,396},{192,756},{384,12},{576,276},{48,444},{240,612},{432,60},{... | collective-permute-start | bytes 2359304 | tf_op jit(solution)/shard_map/ppermute | solution.py:28
  81.4 19.9 %collective-permute-start.3 = (bf16[8,128,384]{2,1,0:T(8,128)(2,1)S(1)}, bf16[8,128,384]{2,1,0:T(8,128)(2,1)S(1)}, u32[]{:S(2)}, u32[]{:S(2)}) collective-permute-start(bf16[8,128,384]{2,1,0:T(8,128)(2,1)S(1)} %collective-permute-done.2.refs_0_), channel_id=1, source_target_pairs={{0,192},{192,0},{384,576},{576,384},{48,240},{240,48},{432,624},{6... | collective-permute-start | bytes 2359304 | tf_op jit(solution)/shard_map/ppermute | solution.py:28
  83.3 7.9 %collective-permute-start = (f32[128,384]{1,0:T(8,128)S(1)}, f32[128,384]{1,0:T(8,128)S(1)}, u32[]{:S(2)}, u32[]{:S(2)}) collective-permute-start(f32[128,384]{1,0:T(8,128)S(1)} %get-tuple-element.11.refs_0_.own_ref), channel_id=1, source_target_pairs={{0,384},{192,576},{384,0},{576,192},{48,432},{240,624},{432,48},{6... | collective-permute-start | bytes 589832 | tf_op jit(solution)/shard_map/ppermute | solution.py:28
  91.2 4.6 %collective-permute-start.1 = (f32[256,384]{1,0:T(8,128)S(1)}, f32[256,384]{1,0:T(8,128)S(1)}, u32[]{:S(2)}, u32[]{:S(2)}) collective-permute-start(f32[256,384]{1,0:T(8,128)S(1)} %join.2), channel_id=1, source_target_pairs={{0,192},{192,0},{384,576},{576,384},{48,240},{240,48},{432,624},{6... | collective-permute-start | bytes 1179656 | tf_op jit(solution)/shard_map/ppermute | solution.py:28
